TPU v7x, 32 devices: a whole 2x2x4 slice. The times are simulated.
32 devices in a mesh: obs: 8 (over z, y), rep: 4 (over x, core).
Axes of the slice: x: 2, y: 2, z: 4, core: 2. Of those that a mesh axis runs over, the one named last changes fastest.
Arguments:
- jacobians: float32 [18, 131072], P(None, ('obs', 'rep')), may hold values from -3 to 3
- residuals: float32 [2, 131072], P(None, ('obs', 'rep')), may hold values from -6 to 6
- camera_local: int32 [131072], P(('obs', 'rep')), may hold values from 0 to 1023
- bucket_counts: int32 [32, 8], P(('obs', 'rep')), may hold values from 1 to 512, as said below
- camera_map: int32 [8192], replicated, may hold values from 0 to 8191, each once
Outputs:
- gradient: float32 [9, 8192], replicated
- camera_blocks: float32 [81, 8192], P(None, 'obs')
Inputs may be any that keep to these rules, and one draw needn't show every extreme that they name: bucket_counts[s, d] counts the leading live slots of bucket d of source block s; exactly one destination d has all 512 slots live from every source block, and every other bucket has at most 256 live slots. A slot in bucket d names camera slot d * 1024 + camera_local. `camera_map`: each camera id appears once.
All inputs are finite; a program needn't handle non-finite values.
Results may differ from a plain program's by a relative error of at most 0.0003.
Values sent between devices are 32-bit elements; how exact they have to be, the bound alone decides.
A program may use at most 192 MiB of HBM per device.

v0:
```python
import functools

import jax
import jax.numpy as jnp
from jax import lax
from jax.experimental import pallas as pl
from jax.experimental.pallas import tpu as pltpu
from jax.sharding import PartitionSpec as P

CAM_DEV = 1024
MESH = pl.DeviceIdType.MESH
F32 = jnp.float32
BF16 = jnp.bfloat16
VMEM = pltpu.VMEM
ROWS = 56
HEAD = 16
KEPT = 48
LOW = 256


def vspec():
    return pl.BlockSpec(memory_space=VMEM)


def split(value):
    high = value.astype(BF16).astype(F32)
    return high, value - high


def pack(counts, jac, res, ids, out):
    buckets = counts.shape[1]
    cap = jac.shape[1] // buckets
    out[0:18, :] = jac[...]
    out[18:20, :] = res[...]
    place = lax.broadcasted_iota(jnp.int32, (1, cap), 1)
    for d in range(buckets):
        lanes = slice(d * cap, (d + 1) * cap)
        out[20:21, lanes] = jnp.where(place < counts[0, d], ids[:, lanes], -1).astype(F32)


def one_hot_of(low, wide):
    shape = (wide, low.shape[1])
    rows = lax.broadcasted_iota(jnp.int32, shape, 0).astype(F32).astype(BF16)
    there = jnp.broadcast_to(low.astype(F32), shape).astype(BF16)
    return jnp.where(there == rows, jnp.ones(shape, BF16), jnp.zeros(shape, BF16))


def add_block(block, terms, acc):
    cap = block.shape[1]
    lead, trail, res = block[0:9], block[9:18], block[18:20]
    ids = block[20:21].astype(jnp.int32)
    at = 9
    for k in range(9):
        terms[at : at + 9 - k, :] = lead[k : k + 1] * lead[k:9] + trail[k : k + 1] * trail[k:9]
        at += 9 - k
    terms[0:9, :] = lead * res[0:1] + trail * res[1:2]
    high, low = split(terms[...])
    both = jnp.concatenate([high, low], axis=0).astype(BF16)
    pieces, _, width = acc.shape
    up = jnp.where(ids < 0, -1, ids // width)
    down = ids - up * width
    one_hot = one_hot_of(down, width)
    up = jnp.broadcast_to(up.astype(F32), both.shape).astype(BF16)
    zero = jnp.zeros_like(both)
    lhs = jnp.concatenate([jnp.where(up == jnp.asarray(h, BF16), both, zero) for h in range(pieces)], axis=0)
    added = lax.dot_general(lhs, one_hot, (((1,), (1,)), ((), ())), preferred_element_type=F32)
    for h in range(pieces):
        at = h * 2 * ROWS
        acc[h] += added[at : at + ROWS] + added[at + ROWS : at + 2 * ROWS]


def expand(blocks, out):
    m, _, width = blocks.shape
    at = 1
    for k in range(9):
        for l in range(k, 9):
            for r in range(m):
                row = blocks[r, at : at + 1, :]
                lanes = slice(r * width, (r + 1) * width)
                out[k * 9 + l : k * 9 + l + 1, lanes] = row
                if l != k:
                    out[l * 9 + k : l * 9 + k + 1, lanes] = row
            at += 1


def place_chunk(o, grads, cmap, ready, acc):
    m, n, _, width = grads.shape
    span = m * width
    highs = n * span // LOW
    slots = jnp.concatenate([grads[r, o] for r in range(m)], axis=1)
    ids = cmap[:, pl.ds(pl.multiple_of(o * span, span), span)]
    up = ids // LOW
    one_hot = one_hot_of(lax.rem(ids, LOW), LOW) if ready is None else ready[o]
    high, low = split(slots)
    top = jnp.concatenate([high[0:8], low[0:8]], axis=0).astype(BF16)
    up16 = jnp.broadcast_to(up.astype(F32), (16, span)).astype(BF16)
    none = jnp.zeros_like(top)
    mask = up == lax.broadcasted_iota(jnp.int32, (highs, span), 0)
    last = jnp.concatenate([jnp.where(mask, high[8:9], 0.0), jnp.where(mask, low[8:9], 0.0)], axis=0).astype(BF16)
    dims = (((1,), (1,)), ((), ()))
    group = min(highs, 32)

    def tiles(start):
        return [jnp.where(up16 == jnp.asarray(start + h, F32).astype(BF16), top, none) for h in range(group)]

    if group == highs:
        lhs = jnp.concatenate(tiles(0) + [last], axis=0)
        acc[...] += lax.dot_general(lhs, one_hot, dims, preferred_element_type=F32)
        return

    def some(g, carry):
        lhs = jnp.concatenate(tiles(g * group), axis=0)
        where = pl.ds(pl.multiple_of(g * group * 16, group * 16), group * 16)
        acc[where, :] += lax.dot_general(lhs, one_hot, dims, preferred_element_type=F32)
        return carry

    lax.fori_loop(0, highs // group, some, 0)
    acc[highs * 16 :, :] += lax.dot_general(last, one_hot, dims, preferred_element_type=F32)


def lay_out(acc, gradient):
    highs = gradient.shape[1] // LOW
    for h in range(highs):
        lanes = slice(h * LOW, (h + 1) * LOW)
        gradient[0:8, lanes] = acc[h * 16 : h * 16 + 8, :] + acc[h * 16 + 8 : h * 16 + 16, :]
        ninth = highs * 16 + h
        gradient[8:9, lanes] = acc[ninth : ninth + 1, :] + acc[ninth + highs : ninth + highs + 1, :]


def main_kernel(
    n, m, counts, jac_in, res_in, ids_in, cmap_in, gradient, out, jac, res, ids, cmap, load_sem, blocks, grads, ready, spread, packed, moved, terms, part, landed, total, mine,
    x_send, x_recv, a_send, a_recv, b_send, b_recv, g_send, g_recv, c_send, c_recv,
):
    me, rep = lax.axis_index("obs"), lax.axis_index("rep")
    width = total.shape[1]
    cap = moved.shape[2]
    barrier = pltpu.get_barrier_semaphore()
    for i in range(1, n):
        pl.semaphore_signal(barrier, inc=1, device_id={"obs": lax.rem(me + i, n)}, device_id_type=MESH)
    for i in range(1, m):
        pl.semaphore_signal(barrier, inc=1, device_id={"rep": lax.rem(rep + i, m)}, device_id_type=MESH)
    pairs = ((jac_in, jac), (res_in, res), (ids_in, ids), (cmap_in, cmap))
    loads = [pltpu.make_async_copy(src, dst, load_sem.at[k]) for k, (src, dst) in enumerate(pairs)]
    for load in loads:
        load.start()
    part[...] = jnp.zeros_like(part)
    terms[...] = jnp.zeros_like(terms)
    spread[...] = jnp.zeros_like(spread)
    for load in loads:
        load.wait()
    pack(counts, jac, res, ids, packed)
    pl.semaphore_wait(barrier, n + m - 2)

    def lanes_of(peer):
        return pl.ds(pl.multiple_of(peer * cap, cap), cap)

    def handing(i):
        peer = lax.rem(me + i, n)
        return pltpu.make_async_remote_copy(
            src_ref=packed.at[:, lanes_of(peer)],
            dst_ref=moved.at[i],
            send_sem=x_send.at[i],
            recv_sem=x_recv.at[i],
            device_id={"obs": peer},
            device_id_type=MESH,
        )

    def start(i, carry):
        handing(i).start()
        return carry

    def take(i, carry):
        handing(i).wait_recv()
        add_block(moved[i], terms, part)
        return carry

    def drain(i, carry):
        handing(i).wait_send()
        return carry

    lax.fori_loop(1, n, start, 0)
    add_block(packed[:, lanes_of(me)], terms, part)
    early = ready.shape[0] == n
    span = m * width

    def prepare(o, carry):
        ids_here = cmap[:, pl.ds(pl.multiple_of(o * span, span), span)]
        ready[o] = one_hot_of(lax.rem(ids_here, LOW), LOW)
        return carry

    if early:
        lax.fori_loop(0, n, prepare, 0)
    lax.fori_loop(1, n, take, 0)

    def send(src, dst, s, r, axis, peer):
        copy = pltpu.make_async_remote_copy(
            src_ref=src, dst_ref=dst, send_sem=s, recv_sem=r, device_id={axis: peer}, device_id_type=MESH
        )
        copy.start()
        return copy

    first, second = [], []
    for half, rows, copies in ((0, pl.ds(0, HEAD), first), (1, pl.ds(HEAD, ROWS - HEAD), second)):
        for i in range(1, m):
            peer = lax.rem(rep + i, m)
            copies.append(
                send(part.at[peer, rows], landed.at[i, rows], a_send.at[half, i], a_recv.at[half, i], "rep", peer)
            )
    for copy in first:
        copy.wait_recv()
    head = part[rep, 0:HEAD]
    for i in range(1, m):
        head = head + landed[i, 0:HEAD]
    mine[...] = head[0:9]
    grads[rep, me] = head[0:9]
    around, wide, across = [], [], {}
    for i in range(1, n):
        peer = lax.rem(me + i, n)
        around.append(send(mine, grads.at[rep, me], g_send.at[i], g_recv.at[i], "obs", peer))
    for j in range(1, m):
        peer = lax.rem(rep + j, m)
        across[j, 0] = send(mine, grads.at[rep, me], c_send.at[j, 0], c_recv.at[j, 0], "rep", peer)
    for copy in second:
        copy.wait_recv()
    rest = part[rep, ROWS - KEPT : ROWS]
    for i in range(1, m):
        rest = rest + landed[i, ROWS - KEPT : ROWS]
    total[...] = rest
    blocks[rep] = rest
    for j in range(1, m):
        peer = lax.rem(rep + j, m)
        wide.append(send(total, blocks.at[rep], b_send.at[j], b_recv.at[j], "rep", peer))
    for copy in first + second:
        copy.wait_send()
    lax.fori_loop(1, n, drain, 0)
    for i in range(1, n):
        around[i - 1].wait_recv()
        source = lax.rem(me - i + n, n)
        for j in range(1, m):
            peer = lax.rem(rep + j, m)
            piece = grads.at[rep, source]
            across[j, i] = send(piece, piece, c_send.at[j, i], c_recv.at[j, i], "rep", peer)
    for copy in wide:
        copy.wait()
    expand(blocks, out)

    def settle(i, carry):
        source = lax.rem(me - i + n, n)
        for j in range(1, m):
            piece = grads.at[rep, source]
            pltpu.make_async_remote_copy(
                src_ref=piece, dst_ref=piece, send_sem=c_send.at[j, i], recv_sem=c_recv.at[j, i],
                device_id={"rep": lax.rem(rep + j, m)}, device_id_type=MESH,
            ).wait_recv()
        place_chunk(source, grads, cmap, ready if early else None, spread)
        return carry

    lax.fori_loop(0, n, settle, 0)
    lay_out(spread, gradient)
    for copy in around:
        copy.wait_send()
    for copy in across.values():
        copy.wait_send()


def write_kernel(gradient, blocks, gradient_out, blocks_out, gradient_held, blocks_held, in_sem, out_sem):
    def cut(ref, count):
        step = ref.shape[1] // count
        return [ref.at[:, pl.ds(c * step, step)] for c in range(count)]

    jobs = list(zip(cut(blocks, 2), cut(blocks_held, 2), cut(blocks_out, 2)))
    jobs += list(zip(cut(gradient, 4), cut(gradient_held, 4), cut(gradient_out, 4)))
    reads = [pltpu.make_async_copy(job[0], job[1], in_sem.at[j]) for j, job in enumerate(jobs)]
    writes = [pltpu.make_async_copy(job[1], job[2], out_sem.at[j]) for j, job in enumerate(jobs)]
    for read in reads:
        read.start()
    for read, write in zip(reads, writes):
        read.wait()
        write.start()
    for write in writes:
        write.wait()


def local(jacobians, residuals, camera_local, bucket_counts, camera_map):
    n, m = lax.axis_size("obs"), lax.axis_size("rep")
    slots = jacobians.shape[1]
    cap = slots // n
    cams = camera_map.shape[0]
    width = CAM_DEV // m
    highs = cams // LOW
    dma = pltpu.SemaphoreType.DMA
    early = n if n * LOW * CAM_DEV * 2 <= 8 * 1024 * 1024 else 1
    limit = 60 * 1024 * 1024
    gradient, out = pl.pallas_call(
        functools.partial(main_kernel, n, m),
        out_shape=(jax.ShapeDtypeStruct((9, cams), F32), jax.ShapeDtypeStruct((81, CAM_DEV), F32)),
        in_specs=[pl.BlockSpec(memory_space=pltpu.SMEM)] + [pl.BlockSpec(memory_space=pltpu.HBM)] * 4,
        out_specs=(vspec(), vspec()),
        scratch_shapes=[
            VMEM((18, slots), F32),
            VMEM((2, slots), F32),
            VMEM((1, slots), jnp.int32),
            VMEM((1, cams), jnp.int32),
            dma((4,)),
            VMEM((m, KEPT, width), F32),
            VMEM((m, n, 9, width), F32),
            VMEM((early, LOW, CAM_DEV), BF16),
            VMEM((highs * 18, LOW), F32),
            VMEM((21, slots), F32),
            VMEM((n, 21, cap), F32),
            VMEM((ROWS, cap), F32),
            VMEM((m, ROWS, width), F32),
            VMEM((m, ROWS, width), F32),
            VMEM((KEPT, width), F32),
            VMEM((9, width), F32),
            dma((n,)),
            dma((n,)),
            dma((2, m)),
            dma((2, m)),
            dma((m,)),
            dma((m,)),
            dma((n,)),
            dma((n,)),
            dma((m, n)),
            dma((m, n)),
        ],
        compiler_params=pltpu.CompilerParams(collective_id=0, has_side_effects=True, vmem_limit_bytes=limit),
    )(bucket_counts, jacobians, residuals, camera_local.reshape(1, slots), camera_map.reshape(1, cams))
    anywhere = pl.BlockSpec(memory_space=pl.ANY)
    shapes = (jax.ShapeDtypeStruct(gradient.shape, F32), jax.ShapeDtypeStruct(out.shape, F32))
    return pl.pallas_call(
        write_kernel,
        out_shape=shapes,
        in_specs=[anywhere] * 2,
        out_specs=(anywhere, anywhere),
        scratch_shapes=[VMEM(gradient.shape, F32), VMEM(out.shape, F32), dma((6,)), dma((6,))],
        compiler_params=pltpu.CompilerParams(vmem_limit_bytes=limit),
    )(gradient, out)


def solution(mesh):
    in_specs = (
        P(None, ("obs", "rep")),
        P(None, ("obs", "rep")),
        P(("obs", "rep")),
        P(("obs", "rep"), None),
        P(),
    )
    out_specs = (P(), P(None, "obs"))
    return jax.shard_map(local, mesh=mesh, in_specs=in_specs, out_specs=out_specs, check_vma=False)
```

profile of v0, /device:TPU:0, one launch (start us, length us, event | category | flops | bytes accessed | tf_op | source)
XLA Modules:
  0.0 36.7 jit_solution(12532392111751617750)
XLA Ops:
  0.6 34.0 %shard_map.68 = (f32[9,8192]{1,0:T(8,128)}, f32[81,1024]{1,0:T(8,128)}) custom-call(s32[1,8]{1,0:T(1,128)} %counts.1, f32[18,4096]{1,0:T(8,128)} %jac_in.1, f32[2,4096]{1,0:T(2,128)} %res_in.1, s32[1,4096]{1,0:T(1,128)} %bitcast.3, s32[1,8192]{1,0:T(1,128)} %bitcast.2), custom_call_target="tpu_custom_call" | custom-call | tf_op jit(solution)/shard_map/pallas_call | solution.py:294
  34.7 2.0 %shard_map.69 = (f32[9,8192]{1,0:T(8,128)}, f32[81,1024]{1,0:T(8,128)}) custom-call(f32[9,8192]{1,0:T(8,128)} %get-tuple-element.4.gradient, f32[81,1024]{1,0:T(8,128)} %get-tuple-element.5.blocks), custom_call_target="tpu_custom_call" | custom-call | tf_op jit(solution)/shard_map/pallas_call | solution.py:331
where the time goes:
time: 36.9 us; the launch traced here: 36.7 us
  Pallas kernels  36.1 us (98%)
  between operations  0.64 us (2%)
    pallas_call x1, Pallas kernels, local(): pl.pallas_call(functools.partial(main_kernel, n, m), out_shape=(jax.Shape...  34 us
    pallas_call x1, Pallas kernels, local(): pl.pallas_call(write_kernel, out_shape=shapes, in_specs=[anywhere] * 2, o...  2.01 us

commit v1 on v0

v1 whole, which is shorter than its diff:
```python
import functools

import jax
import jax.numpy as jnp
from jax import lax
from jax.experimental import pallas as pl
from jax.experimental.pallas import tpu as pltpu
from jax.sharding import PartitionSpec as P

CAM_DEV = 1024
MESH = pl.DeviceIdType.MESH
F32 = jnp.float32
BF16 = jnp.bfloat16
VMEM = pltpu.VMEM
KEPT = 48
LOW = 256
PAIR = 2
EARLY = 3
MIB = 1024 * 1024
DIMS = (((1,), (1,)), ((), ()))


def vspec():
    return pl.BlockSpec(memory_space=VMEM)


def xor(a, b, size):
    out, bit = 0, 1
    while bit < size:
        p, q = lax.rem(a // bit, 2), lax.rem(b // bit, 2)
        out = out + bit * (p + q - 2 * p * q)
        bit *= 2
    return out


def split(value):
    high = value.astype(BF16).astype(F32)
    return high, value - high


def pack(counts, jac, res, ids, own8, own2, tail):
    buckets = counts.shape[1]
    cap = jac.shape[1] // buckets
    tail[...] = jac[16:18, :]
    own8[...] = jac[0:8, :] * res[0:1, :] + jac[9:17, :] * res[1:2, :]
    own2[0:1, :] = jac[8:9, :] * res[0:1, :] + jac[17:18, :] * res[1:2, :]
    place = lax.broadcasted_iota(jnp.int32, (1, cap), 1)
    for d in range(buckets):
        lanes = slice(d * cap, (d + 1) * cap)
        own2[1:2, lanes] = jnp.where(place < counts[0, d], ids[:, lanes], -1).astype(F32)


def one_hot_of(low, wide):
    shape = (wide, low.shape[1])
    rows = lax.broadcasted_iota(jnp.int32, shape, 0).astype(F32).astype(BF16)
    there = jnp.broadcast_to(low.astype(F32), shape).astype(BF16)
    return jnp.where(there == rows, jnp.ones(shape, BF16), jnp.zeros(shape, BF16))


def place_of(pair, width):
    ids = pair[1:2].astype(jnp.int32)
    up = jnp.where(ids < 0, -1, ids // width)
    return up, ids - up * width


def masked_tiles(value, up, pieces):
    up = jnp.broadcast_to(up.astype(F32), value.shape).astype(BF16)
    zero = jnp.zeros_like(value)
    return [jnp.where(up == jnp.asarray(h, BF16), value, zero) for h in range(pieces)]


def add_gradient(eight, pair, hot, acc, pieces):
    up, down = place_of(pair, acc.shape[1])
    one_hot = one_hot_of(down, acc.shape[1])
    if hot is not None:
        hot[...] = one_hot
    high, low = split(eight)
    tiles = masked_tiles(jnp.concatenate([high, low], axis=0).astype(BF16), up, pieces)
    high, low = split(pair[0:1])
    mask = up == lax.broadcasted_iota(jnp.int32, (pieces, up.shape[1]), 0)
    last = jnp.concatenate([jnp.where(mask, high, 0.0), jnp.where(mask, low, 0.0)], axis=0).astype(BF16)
    lhs = jnp.concatenate(tiles + [last], axis=0)
    acc[...] += lax.dot_general(lhs, one_hot, DIMS, preferred_element_type=F32)


def add_block(most, tail, pair, hot, terms, acc):
    pieces, _, width = acc.shape
    lead, trail = most[0:9], jnp.concatenate([most[9:16], tail], axis=0)
    at = 0
    for k in range(9):
        terms[at : at + 9 - k, :] = lead[k : k + 1] * lead[k:9] + trail[k : k + 1] * trail[k:9]
        at += 9 - k
    high, low = split(terms[...])
    both = jnp.concatenate([high, low], axis=0).astype(BF16)
    up, down = place_of(pair, width)
    one_hot = one_hot_of(down, width) if hot is None else hot[...]
    lhs = jnp.concatenate(masked_tiles(both, up, pieces), axis=0)
    added = lax.dot_general(lhs, one_hot, DIMS, preferred_element_type=F32)
    for h in range(pieces):
        at = h * 2 * KEPT
        acc[h] += added[at : at + KEPT] + added[at + KEPT : at + 2 * KEPT]


def expand(blocks, out):
    m, _, width = blocks.shape
    at = 0
    for k in range(9):
        for l in range(k, 9):
            for r in range(m):
                row = blocks[r, at : at + 1, :]
                lanes = slice(r * width, (r + 1) * width)
                out[k * 9 + l : k * 9 + l + 1, lanes] = row
                if l != k:
                    out[l * 9 + k : l * 9 + k + 1, lanes] = row
            at += 1


def place_chunk(o, grads8, grads9, cmap, ready, acc):
    m, n, _, width = grads8.shape
    span = m * width
    highs = n * span // LOW
    eight = jnp.concatenate([grads8[r, o] for r in range(m)], axis=1)
    ninth = jnp.concatenate([grads9[r, o] for r in range(m)], axis=1)
    ids = cmap[:, pl.ds(pl.multiple_of(o * span, span), span)]
    up = ids // LOW
    one_hot = one_hot_of(lax.rem(ids, LOW), LOW) if ready is None else ready[o]
    high, low = split(eight)
    top = jnp.concatenate([high, low], axis=0).astype(BF16)
    up16 = jnp.broadcast_to(up.astype(F32), (16, span)).astype(BF16)
    none = jnp.zeros_like(top)
    mask = up == lax.broadcasted_iota(jnp.int32, (highs, span), 0)
    high, low = split(ninth)
    last = jnp.concatenate([jnp.where(mask, high, 0.0), jnp.where(mask, low, 0.0)], axis=0).astype(BF16)
    group = min(highs, 32)

    def tiles(start):
        return [jnp.where(up16 == jnp.asarray(start + h, F32).astype(BF16), top, none) for h in range(group)]

    if group == highs:
        lhs = jnp.concatenate(tiles(0) + [last], axis=0)
        acc[...] += lax.dot_general(lhs, one_hot, DIMS, preferred_element_type=F32)
        return

    def some(g, carry):
        lhs = jnp.concatenate(tiles(g * group), axis=0)
        where = pl.ds(pl.multiple_of(g * group * 16, group * 16), group * 16)
        acc[where, :] += lax.dot_general(lhs, one_hot, DIMS, preferred_element_type=F32)
        return carry

    lax.fori_loop(0, highs // group, some, 0)
    acc[highs * 16 :, :] += lax.dot_general(last, one_hot, DIMS, preferred_element_type=F32)


def lay_out(acc, gradient):
    highs = gradient.shape[1] // LOW
    for h in range(highs):
        lanes = slice(h * LOW, (h + 1) * LOW)
        gradient[0:8, lanes] = acc[h * 16 : h * 16 + 8, :] + acc[h * 16 + 8 : h * 16 + 16, :]
        ninth = highs * 16 + h
        gradient[8:9, lanes] = acc[ninth : ninth + 1, :] + acc[ninth + highs : ninth + highs + 1, :]


def main_kernel(
    n, m, counts, jac_in, res_in, ids_in, cmap_in, gradient, out, jac, res, ids, cmap, load_sem,
    own8, own2, tail, got8, got2, got16, got_tail, hots, terms, part, landed, total, blocks,
    gsum, part8, part9, land8, land9, mine8, mine9, grads8, grads9, ready, spread,
    x_send, x_recv, a_send, a_recv, g_send, g_recv, c_send, c_recv, b_send, b_recv, w_send, w_recv,
):
    me, rep = lax.axis_index("obs"), lax.axis_index("rep")
    width = total.shape[1]
    cap = got8.shape[2]
    half = m // PAIR
    sibling = rep + 1 - 2 * lax.rem(rep, PAIR)
    barrier = pltpu.get_barrier_semaphore()

    def greet(i, carry):
        for j in range(half):
            where = {"obs": xor(me, i, n), "rep": lax.rem(rep + PAIR * j, m)}
            pl.semaphore_signal(barrier, inc=1, device_id=where, device_id_type=MESH)
        return carry

    lax.fori_loop(1, n, greet, 0)
    for i in range(1, m):
        pl.semaphore_signal(barrier, inc=1, device_id={"rep": lax.rem(rep + i, m)}, device_id_type=MESH)
    pairs = ((jac_in, jac), (res_in, res), (ids_in, ids), (cmap_in, cmap))
    loads = [pltpu.make_async_copy(src, dst, load_sem.at[k]) for k, (src, dst) in enumerate(pairs)]
    for load in loads:
        load.start()
    part[...] = jnp.zeros_like(part)
    terms[...] = jnp.zeros_like(terms)
    gsum[...] = jnp.zeros_like(gsum)
    spread[...] = jnp.zeros_like(spread)
    for load in loads:
        load.wait()
    pack(counts, jac, res, ids, own8, own2, tail)
    pl.semaphore_wait(barrier, (n - 1) * half + m - 1)

    def lanes_of(peer):
        return pl.ds(pl.multiple_of(peer * cap, cap), cap)

    def handing(i, kinds):
        peer = xor(me, i, n)
        lanes = lanes_of(peer)
        sent = (own8.at[:, lanes], own2.at[:, lanes], jac.at[0:16, lanes], tail.at[:, lanes])
        taken = (got8.at[i], got2.at[i], got16.at[i], got_tail.at[i])
        return [
            pltpu.make_async_remote_copy(
                src_ref=sent[k], dst_ref=taken[k], send_sem=x_send.at[k, i], recv_sem=x_recv.at[k, i],
                device_id={"obs": peer}, device_id_type=MESH,
            )
            for k in kinds
        ]

    def start(kinds):
        def one(i, carry):
            for copy in handing(n - i, kinds):
                copy.start()
            return carry

        lax.fori_loop(1, n, one, 0)

    start((0, 1))
    start((2, 3))
    early = ready.shape[0] == n

    def hot_at(i):
        return hots.at[i] if early else None

    def prepare(o, carry):
        ids_here = cmap[:, pl.ds(pl.multiple_of(o * m * width, m * width), m * width)]
        ready[o] = one_hot_of(lax.rem(ids_here, LOW), LOW)
        return carry

    def take_gradient(i, carry):
        for copy in handing(i, (0, 1)):
            copy.wait_recv()
        add_gradient(got8[i], got2[i], hot_at(i), gsum, m)
        return carry

    def take_block(i, carry):
        for copy in handing(i, (2, 3)):
            copy.wait_recv()
        add_block(got16[i], got_tail[i], got2[i], hot_at(i), terms, part)
        return carry

    mylanes = lanes_of(me)
    add_gradient(own8[:, mylanes], own2[:, mylanes], hot_at(0), gsum, m)
    if early:
        lax.fori_loop(0, n, prepare, 0)
    lax.fori_loop(1, n, take_gradient, 0)
    for h in range(m):
        part8[h] = gsum[h * 16 : h * 16 + 8, :] + gsum[h * 16 + 8 : h * 16 + 16, :]
        ninth = m * 16 + h
        part9[h] = gsum[ninth : ninth + 1, :] + gsum[ninth + m : ninth + m + 1, :]

    def to_rep(src, dst, s, r, peer):
        return pltpu.make_async_remote_copy(
            src_ref=src, dst_ref=dst, send_sem=s, recv_sem=r, device_id={"rep": peer}, device_id_type=MESH
        )

    heads = []
    for i in range(1, m):
        peer = lax.rem(rep + i, m)
        heads.append(to_rep(part8.at[peer], land8.at[i], a_send.at[0, i], a_recv.at[0, i], peer))
        heads.append(to_rep(part9.at[peer], land9.at[i], a_send.at[1, i], a_recv.at[1, i], peer))
    for copy in heads:
        copy.start()
    add_block(jac[0:16, mylanes], tail[:, mylanes], own2[:, mylanes], hot_at(0), terms, part)
    lax.fori_loop(1, min(EARLY, n), take_block, 0)
    for copy in heads:
        copy.wait_recv()
    eight, ninth = part8[rep], part9[rep]
    for i in range(1, m):
        eight = eight + land8[i]
        ninth = ninth + land9[i]
    mine8[...] = eight
    mine9[...] = ninth
    grads8[rep, me] = eight
    grads9[rep, me] = ninth

    def at_origin(origin, source):
        return grads8.at[origin, source], grads9.at[origin, source]

    def reach(i, j):
        where = {"obs": xor(me, i, n), "rep": lax.rem(rep + PAIR * j, m)}
        return [
            pltpu.make_async_remote_copy(
                src_ref=src, dst_ref=dst, send_sem=g_send.at[k, i, j], recv_sem=g_recv.at[k, i, j],
                device_id=where, device_id_type=MESH,
            )
            for k, (src, dst) in enumerate(zip((mine8, mine9), at_origin(rep, me)))
        ]

    def hand_over(i, j, src, dst):
        return [to_rep(src[k], dst[k], c_send.at[k, i, j], c_recv.at[k, i, j], sibling) for k in range(2)]

    def spread_out(i, carry):
        for j in reversed(range(half)):
            for copy in reach(n - i, j):
                copy.start()
        return carry

    lax.fori_loop(1, n, spread_out, 0)
    for j in range(1, half):
        for copy in reach(0, j):
            copy.start()
    for copy in hand_over(0, 0, (mine8, mine9), at_origin(rep, me)):
        copy.start()
    lax.fori_loop(min(EARLY, n), n, take_block, 0)
    folds = []
    for i in range(1, m):
        peer = lax.rem(rep + i, m)
        folds.append(to_rep(part.at[peer], landed.at[i], b_send.at[i], b_recv.at[i], peer))
    for copy in folds:
        copy.start()

    def relay(i, first):
        source = xor(me, i, n)
        for j in range(first, half):
            for copy in reach(i, j):
                copy.wait_recv()
            piece = at_origin(lax.rem(rep - PAIR * j + m, m), source)
            for copy in hand_over(i, j, piece, piece):
                copy.start()

    def relay_all(i, carry):
        relay(i, 0)
        return carry

    def place(i, carry):
        source = xor(me, i, n)
        for j in range(half):
            piece = at_origin(lax.rem(sibling - PAIR * j + m, m), source)
            for copy in hand_over(i, j, piece, piece):
                copy.wait_recv()
        place_chunk(source, grads8, grads9, cmap, ready if early else None, spread)
        return carry

    relay(0, 1)
    for copy in folds:
        copy.wait_recv()
    rest = part[rep]
    for i in range(1, m):
        rest = rest + landed[i]
    total[...] = rest
    blocks[rep] = rest
    wide = []
    for j in range(1, m):
        peer = lax.rem(rep + j, m)
        wide.append(to_rep(total, blocks.at[rep], w_send.at[j], w_recv.at[j], peer))
    for copy in wide:
        copy.start()
    lax.fori_loop(1, n, relay_all, 0)
    lax.fori_loop(0, n, place, 0)
    lay_out(spread, gradient)
    for copy in wide:
        copy.wait_recv()
    expand(blocks, out)

    def finish(i, carry):
        for j in range(half):
            piece = at_origin(rep, me)
            for copy in hand_over(i, j, piece, piece):
                copy.wait_send()
        return carry

    def finish_far(i, carry):
        for copy in handing(i, (0, 1, 2, 3)):
            copy.wait_send()
        for j in range(half):
            for copy in reach(i, j):
                copy.wait_send()
        return carry

    lax.fori_loop(0, n, finish, 0)
    lax.fori_loop(1, n, finish_far, 0)
    for j in range(1, half):
        for copy in reach(0, j):
            copy.wait_send()
    for copy in heads + folds + wide:
        copy.wait_send()


def write_kernel(gradient, blocks, gradient_out, blocks_out, out_sem):
    def cut(ref, count):
        step = ref.shape[1] // count
        return [ref.at[:, pl.ds(c * step, step)] for c in range(count)]

    jobs = list(zip(cut(blocks, 2), cut(blocks_out, 2)))
    jobs += list(zip(cut(gradient, 4), cut(gradient_out, 4)))
    writes = [pltpu.make_async_copy(job[0], job[1], out_sem.at[j]) for j, job in enumerate(jobs)]
    for write in writes:
        write.start()
    for write in writes:
        write.wait()


def local(jacobians, residuals, camera_local, bucket_counts, camera_map):
    n, m = lax.axis_size("obs"), lax.axis_size("rep")
    slots = jacobians.shape[1]
    cap = slots // n
    cams = camera_map.shape[0]
    width = CAM_DEV // m
    highs = cams // LOW
    half = m // PAIR
    dma = pltpu.SemaphoreType.DMA
    early = n * LOW * CAM_DEV * 2 <= 8 * MIB
    kept = n if early else 1
    held = 16 * cams * 4 + 88 * CAM_DEV * 4
    limit = 60 * MIB - max(0, held - 2 * MIB)
    gradient, out = pl.pallas_call(
        functools.partial(main_kernel, n, m),
        out_shape=(VMEM((9, cams), F32), VMEM((81, CAM_DEV), F32)),
        in_specs=[pl.BlockSpec(memory_space=pltpu.SMEM)] + [pl.BlockSpec(memory_space=pltpu.HBM)] * 4,
        out_specs=(vspec(), vspec()),
        scratch_shapes=[
            VMEM((18, slots), F32),
            VMEM((2, slots), F32),
            VMEM((1, slots), jnp.int32),
            VMEM((1, cams), jnp.int32),
            dma((4,)),
            VMEM((8, slots), F32),
            VMEM((2, slots), F32),
            VMEM((2, slots), F32),
            VMEM((n, 8, cap), F32),
            VMEM((n, 2, cap), F32),
            VMEM((n, 16, cap), F32),
            VMEM((n, 2, cap), F32),
            VMEM((kept, width, cap), BF16),
            VMEM((KEPT, cap), F32),
            VMEM((m, KEPT, width), F32),
            VMEM((m, KEPT, width), F32),
            VMEM((KEPT, width), F32),
            VMEM((m, KEPT, width), F32),
            VMEM((m * 18, width), F32),
            VMEM((m, 8, width), F32),
            VMEM((m, 1, width), F32),
            VMEM((m, 8, width), F32),
            VMEM((m, 1, width), F32),
            VMEM((8, width), F32),
            VMEM((1, width), F32),
            VMEM((m, n, 8, width), F32),
            VMEM((m, n, 1, width), F32),
            VMEM((kept, LOW, CAM_DEV), BF16),
            VMEM((highs * 18, LOW), F32),
            dma((4, n)),
            dma((4, n)),
            dma((2, m)),
            dma((2, m)),
            dma((2, n, half)),
            dma((2, n, half)),
            dma((2, n, half)),
            dma((2, n, half)),
            dma((m,)),
            dma((m,)),
            dma((m,)),
            dma((m,)),
        ],
        compiler_params=pltpu.CompilerParams(collective_id=0, has_side_effects=True, vmem_limit_bytes=limit),
    )(bucket_counts, jacobians, residuals, camera_local.reshape(1, slots), camera_map.reshape(1, cams))
    anywhere = pl.BlockSpec(memory_space=pl.ANY)
    shapes = (jax.ShapeDtypeStruct(gradient.shape, F32), jax.ShapeDtypeStruct(out.shape, F32))
    return pl.pallas_call(
        write_kernel,
        out_shape=shapes,
        in_specs=[vspec()] * 2,
        out_specs=(anywhere, anywhere),
        scratch_shapes=[dma((6,))],
        compiler_params=pltpu.CompilerParams(vmem_limit_bytes=2 * MIB),
    )(gradient, out)


def solution(mesh):
    in_specs = (
        P(None, ("obs", "rep")),
        P(None, ("obs", "rep")),
        P(("obs", "rep")),
        P(("obs", "rep"), None),
        P(),
    )
    out_specs = (P(), P(None, "obs"))
    return jax.shard_map(local, mesh=mesh, in_specs=in_specs, out_specs=out_specs, check_vma=False)
```

time: 36.9 us -> 33.9 us (0.919)
  Pallas kernels: 36.1 us -> 33.2 us
    pallas_call x2, Pallas kernels: 36.1 us -> 33.2 us  [the longest x1 32.2 us: local(): pl.pallas_call(functools.partial(main_kernel, n, m), out_shape=(VMEM((9,...]
where the time goes in v1:
time: 33.9 us; the launch traced here: 33.8 us
  Pallas kernels  33.2 us (98%)
  between operations  0.64 us (2%)
    pallas_call x1, Pallas kernels, local(): pl.pallas_call(functools.partial(main_kernel, n, m), out_shape=(VMEM((9,...  32.2 us
    pallas_call x1, Pallas kernels, local(): pl.pallas_call(write_kernel, out_shape=shapes, in_specs=[vspec()] * 2, ou...  0.96 us

profile of v1, /device:TPU:0, one launch (start us, length us, event | category | flops | bytes accessed | tf_op | source)
XLA Modules:
  0.0 33.8 jit_solution(9784704369511332830)
XLA Ops:
  0.6 32.2 %shard_map.68 = (f32[9,8192]{1,0:T(8,128)S(1)}, f32[81,1024]{1,0:T(8,128)S(1)}) custom-call(s32[1,8]{1,0:T(1,128)} %counts.1, f32[18,4096]{1,0:T(8,128)} %jac_in.1, f32[2,4096]{1,0:T(2,128)} %res_in.1, s32[1,4096]{1,0:T(1,128)} %bitcast.3, s32[1,8192]{1,0:T(1,128)} %bitcast.2), custom_call_target="tpu_custom_call" | custom-call | tf_op jit(solution)/shard_map/pallas_call | solution.py:411
  32.8 1.0 %shard_map.69 = (f32[9,8192]{1,0:T(8,128)}, f32[81,1024]{1,0:T(8,128)}) custom-call(f32[9,8192]{1,0:T(8,128)S(1)} %get-tuple-element.4.gradient, f32[81,1024]{1,0:T(8,128)S(1)} %get-tuple-element.5.blocks), custom_call_target="tpu_custom_call" | custom-call | tf_op jit(solution)/shard_map/pallas_call | solution.py:463

commit v2 on v1

v2 whole, which is shorter than its diff:
```python
import functools

import jax
import jax.numpy as jnp
from jax import lax
from jax.experimental import pallas as pl
from jax.experimental.pallas import tpu as pltpu
from jax.sharding import PartitionSpec as P

CAM_DEV = 1024
MESH = pl.DeviceIdType.MESH
F32 = jnp.float32
BF16 = jnp.bfloat16
VMEM = pltpu.VMEM
ROWS = 56
KEPT = 48
CUTS = 4
LOW = 256
PAIR = 2
MIB = 1024 * 1024
DIMS = (((1,), (1,)), ((), ()))


def vspec():
    return pl.BlockSpec(memory_space=VMEM)


def flipper(me, size):
    weights = [1 << k for k in range(size.bit_length() - 1)]
    signed = [w * (1 - 2 * lax.rem(me // w, 2)) for w in weights]

    def flip(i):
        out = me
        for w, s in zip(weights, signed):
            if isinstance(i, int):
                out = out + s if i // w % 2 else out
            else:
                out = out + s * lax.rem(lax.div(i, w), 2)
        return out

    return flip


def each(first, last, body):
    if last - first <= 8:
        for i in range(first, last):
            body(i)
    else:
        lax.fori_loop(first, last, lambda i, carry: (body(i), carry)[1], 0)


def split(value):
    high = value.astype(BF16).astype(F32)
    return high, value - high


def pack(counts, jac, res, ids, own4, own1):
    buckets = counts.shape[1]
    cap = jac.shape[1] // buckets
    own4[0:2, :] = jac[16:18, :]
    own4[2:4, :] = res[...]
    place = lax.broadcasted_iota(jnp.int32, (1, cap), 1)
    for d in range(buckets):
        lanes = slice(d * cap, (d + 1) * cap)
        own1[:, lanes] = jnp.where(place < counts[0, d], ids[:, lanes], -1).astype(F32)


def one_hot_of(low, wide):
    shape = (wide, low.shape[1])
    rows = lax.broadcasted_iota(jnp.int32, shape, 0).astype(F32).astype(BF16)
    there = jnp.broadcast_to(low.astype(F32), shape).astype(BF16)
    return jnp.where(there == rows, jnp.ones(shape, BF16), jnp.zeros(shape, BF16))


def place_of(ids, width):
    ids = ids.astype(jnp.int32)
    up = jnp.where(ids < 0, -1, ids // width)
    return up, ids - up * width


def masked_tiles(value, up, pieces):
    up = jnp.broadcast_to(up.astype(F32), value.shape).astype(BF16)
    zero = jnp.zeros_like(value)
    return [jnp.where(up == jnp.asarray(h, BF16), value, zero) for h in range(pieces)]


def add_block(most, four, ids, hot, terms, acc):
    pieces, _, width = acc.shape
    lead, trail, res = most[0:9], jnp.concatenate([most[9:16], four[0:2]], axis=0), four[2:4]
    at = 9
    for k in range(9):
        terms[at : at + 9 - k, :] = lead[k : k + 1] * lead[k:9] + trail[k : k + 1] * trail[k:9]
        at += 9 - k
    terms[0:9, :] = lead * res[0:1] + trail * res[1:2]
    high, low = split(terms[...])
    both = jnp.concatenate([high, low], axis=0).astype(BF16)
    up, down = place_of(ids, width)
    one_hot = one_hot_of(down, width) if hot is None else hot[...]
    lhs = jnp.concatenate(masked_tiles(both, up, pieces), axis=0)
    added = lax.dot_general(lhs, one_hot, DIMS, preferred_element_type=F32)
    for h in range(pieces):
        at = h * 2 * ROWS
        acc[h] += added[at : at + ROWS] + added[at + ROWS : at + 2 * ROWS]


def expand(blocks, out):
    m, _, width = blocks.shape
    at = 1
    for k in range(9):
        for l in range(k, 9):
            for r in range(m):
                row = blocks[r, at : at + 1, :]
                lanes = slice(r * width, (r + 1) * width)
                out[k * 9 + l : k * 9 + l + 1, lanes] = row
                if l != k:
                    out[l * 9 + k : l * 9 + k + 1, lanes] = row
            at += 1


def side_ids(o, side, pieces, cmap, width):
    m = PAIR * pieces

    def at(j):
        return pl.ds(pl.multiple_of((o * m + side + PAIR * j) * width, width), width)

    return jnp.concatenate([cmap[:, at(j)] for j in range(pieces)], axis=1)


def place_chunk(eight, ninth, ids, one_hot, acc):
    span = ids.shape[1]
    highs = acc.shape[0] // 18
    up = ids // LOW
    if one_hot is None:
        one_hot = one_hot_of(lax.rem(ids, LOW), LOW)
    high, low = split(eight)
    top = jnp.concatenate([high, low], axis=0).astype(BF16)
    up16 = jnp.broadcast_to(up.astype(F32), (16, span)).astype(BF16)
    none = jnp.zeros_like(top)
    mask = up == lax.broadcasted_iota(jnp.int32, (highs, span), 0)
    high, low = split(ninth)
    last = jnp.concatenate([jnp.where(mask, high, 0.0), jnp.where(mask, low, 0.0)], axis=0).astype(BF16)
    group = min(highs, 32)

    def tiles(start):
        return [jnp.where(up16 == jnp.asarray(start + h, F32).astype(BF16), top, none) for h in range(group)]

    if group == highs:
        lhs = jnp.concatenate(tiles(0) + [last], axis=0)
        acc[...] += lax.dot_general(lhs, one_hot, DIMS, preferred_element_type=F32)
        return

    def some(g, carry):
        lhs = jnp.concatenate(tiles(g * group), axis=0)
        where = pl.ds(pl.multiple_of(g * group * 16, group * 16), group * 16)
        acc[where, :] += lax.dot_general(lhs, one_hot, DIMS, preferred_element_type=F32)
        return carry

    lax.fori_loop(0, highs // group, some, 0)
    acc[highs * 16 :, :] += lax.dot_general(last, one_hot, DIMS, preferred_element_type=F32)


def lay_out(acc, out8, out9, first, last):
    highs = out8.shape[1] // LOW
    for h in range(first, last):
        lanes = slice(h * LOW, (h + 1) * LOW)
        out8[:, lanes] = acc[h * 16 : h * 16 + 8, :] + acc[h * 16 + 8 : h * 16 + 16, :]
        ninth = highs * 16 + h
        out9[:, lanes] = acc[ninth : ninth + 1, :] + acc[ninth + highs : ninth + highs + 1, :]


def main_kernel(
    n, m, counts, jac_in, res_in, ids_in, cmap_in, gradient, out, jac, res, ids, cmap, load_sem,
    own4, own1, got16, got4, got1, hots, terms, part, fold, landed, total, blocks,
    part8, part9, land8, land9, mine8, mine9, grads8, grads9, ready, spread, out8, out9, sib8, sib9,
    x_send, x_recv, a_send, a_recv, g_send, g_recv, c_send, c_recv, b_send, b_recv, w_send, w_recv, d_send, d_recv,
):
    me, rep = lax.axis_index("obs"), lax.axis_index("rep")
    width = total.shape[2]
    cap = got16.shape[2]
    half = m // PAIR
    sibling = rep + 1 - 2 * lax.rem(rep, PAIR)
    barrier = pltpu.get_barrier_semaphore()

    flip = flipper(me, n)

    def greet(i):
        pl.semaphore_signal(barrier, inc=1, device_id={"obs": flip(i)}, device_id_type=MESH)

    each(1, n, greet)
    for i in range(1, m):
        pl.semaphore_signal(barrier, inc=1, device_id={"rep": lax.rem(rep + i, m)}, device_id_type=MESH)
    pairs = ((jac_in, jac), (res_in, res), (ids_in, ids), (cmap_in, cmap))
    loads = [pltpu.make_async_copy(src, dst, load_sem.at[k]) for k, (src, dst) in enumerate(pairs)]
    for load in loads:
        load.start()
    part[...] = jnp.zeros_like(part)
    terms[...] = jnp.zeros_like(terms)
    spread[...] = jnp.zeros_like(spread)
    for load in loads:
        load.wait()
    pack(counts, jac, res, ids, own4, own1)
    pl.semaphore_wait(barrier, n + m - 2)

    def lanes_of(peer):
        return pl.ds(pl.multiple_of(peer * cap, cap), cap)

    def handing(i, kinds):
        peer = flip(i)
        lanes = lanes_of(peer)
        sent = (own1.at[:, lanes], jac.at[0:16, lanes], own4.at[:, lanes])
        taken = (got1.at[i], got16.at[i], got4.at[i])
        return [
            pltpu.make_async_remote_copy(
                src_ref=sent[k], dst_ref=taken[k], send_sem=x_send.at[k, i], recv_sem=x_recv.at[k, i],
                device_id={"obs": peer}, device_id_type=MESH,
            )
            for k in kinds
        ]

    def start(kinds):
        def one(i):
            for copy in handing(n - i, kinds):
                copy.start()

        each(1, n, one)

    start((0,))
    start((1, 2))
    early = ready.shape[0] == n

    def hot_at(i):
        return hots.at[i] if early else None

    side = lax.rem(rep, PAIR)

    def prepare(o, carry):
        ready[o] = one_hot_of(lax.rem(side_ids(o, side, half, cmap, width), LOW), LOW)
        return carry

    def foresee(i, carry):
        for copy in handing(i, (0,)):
            copy.wait_recv()
        if early:
            hots[i] = one_hot_of(place_of(got1[i], width)[1], width)
        return carry

    def take(i, carry):
        for copy in handing(i, (1, 2)):
            copy.wait_recv()
        add_block(got16[i], got4[i], got1[i], hot_at(i), terms, part)
        return carry

    mylanes = lanes_of(me)
    add_block(jac[0:16, mylanes], own4[:, mylanes], own1[:, mylanes], None, terms, part)
    lax.fori_loop(1, n, foresee, 0)
    if early:
        lax.fori_loop(0, n, prepare, 0)
    lax.fori_loop(1, n, take, 0)
    for h in range(m):
        part8[h] = part[h, 0:8]
        part9[h] = part[h, 8:9]

    def to_rep(src, dst, s, r, peer):
        return pltpu.make_async_remote_copy(
            src_ref=src, dst_ref=dst, send_sem=s, recv_sem=r, device_id={"rep": peer}, device_id_type=MESH
        )

    heads = []
    for i in range(1, m):
        peer = lax.rem(rep + i, m)
        heads.append(to_rep(part8.at[peer], land8.at[i], a_send.at[0, i], a_recv.at[0, i], peer))
        heads.append(to_rep(part9.at[peer], land9.at[i], a_send.at[1, i], a_recv.at[1, i], peer))
    for copy in heads:
        copy.start()
    mine_at, other_at = side * half, (1 - side) * half
    folds, wide, back = [], [], []
    for h in range(half):
        folds.append(to_rep(part.at[other_at + h, pl.ds(ROWS - KEPT, KEPT)], fold.at[h], b_send.at[h], b_recv.at[h], sibling))
        for j in range(1, half):
            peer = lax.rem(rep + PAIR * j, m)
            wide.append(to_rep(total.at[h], landed.at[j, h], w_send.at[j, h], w_recv.at[j, h], peer))
        back.append(to_rep(blocks.at[mine_at + h], blocks.at[mine_at + h], d_send.at[h], d_recv.at[h], sibling))
    for copy in folds:
        copy.start()
    for copy in heads:
        copy.wait_recv()
    eight, ninth = part8[rep], part9[rep]
    for i in range(1, m):
        eight = eight + land8[i]
        ninth = ninth + land9[i]
    mine8[...] = eight
    mine9[...] = ninth
    grads8[lax.div(rep, PAIR), me] = eight
    grads9[lax.div(rep, PAIR), me] = ninth

    def at_origin(origin, source):
        return grads8.at[origin, source], grads9.at[origin, source]

    def reach(i, j):
        where = {"obs": flip(i), "rep": lax.rem(rep + PAIR * j, m)}
        return [
            pltpu.make_async_remote_copy(
                src_ref=src, dst_ref=dst, send_sem=g_send.at[k, i, j], recv_sem=g_recv.at[k, i, j],
                device_id=where, device_id_type=MESH,
            )
            for k, (src, dst) in enumerate(zip((mine8, mine9), at_origin(lax.div(rep, PAIR), me)))
        ]

    def spread_out(i):
        for j in reversed(range(half)):
            for copy in reach(n - i, j):
                copy.start()

    each(1, n, spread_out)
    for j in range(1, half):
        for copy in reach(0, j):
            copy.start()

    def place(i, first):
        source = flip(i)
        for j in range(first, half):
            for copy in reach(i, j):
                copy.wait_recv()
        eight = jnp.concatenate([grads8[j, source] for j in range(half)], axis=1)
        ninth = jnp.concatenate([grads9[j, source] for j in range(half)], axis=1)
        here = side_ids(source, side, half, cmap, width)
        place_chunk(eight, ninth, here, ready[source] if early else None, spread)

    def settle(i, carry):
        place(i, 0)
        return carry

    for h in range(half):
        folds[h].wait_recv()
        total[h] = part[mine_at + h, ROWS - KEPT :] + fold[h]
        for copy in wide[h * (half - 1) : (h + 1) * (half - 1)]:
            copy.start()
    place(0, 1)
    lax.fori_loop(1, n, settle, 0)
    swaps = []
    highs, step = gradient.shape[1] // LOW, gradient.shape[1] // CUTS
    for c in range(CUTS):
        lanes = pl.ds(c * step, step)
        lay_out(spread, out8, out9, c * highs // CUTS, (c + 1) * highs // CUTS)
        swaps.append(to_rep(out8.at[:, lanes], sib8.at[:, lanes], c_send.at[0, c], c_recv.at[0, c], sibling))
        swaps.append(to_rep(out9.at[:, lanes], sib9.at[:, lanes], c_send.at[1, c], c_recv.at[1, c], sibling))
        for copy in swaps[-2:]:
            copy.start()
    for h in range(half):
        for copy in wide[h * (half - 1) : (h + 1) * (half - 1)]:
            copy.wait_recv()
        full = total[h]
        for j in range(1, half):
            full = full + landed[j, h]
        blocks[mine_at + h] = full
        back[h].start()
    for c in range(CUTS):
        lanes = slice(c * step, (c + 1) * step)
        for copy in swaps[2 * c : 2 * c + 2]:
            copy.wait_recv()
        gradient[0:8, lanes] = out8[:, lanes] + sib8[:, lanes]
        gradient[8:9, lanes] = out9[:, lanes] + sib9[:, lanes]
    for copy in back:
        copy.wait_recv()
    expand(blocks, out)

    def finish(i):
        for copy in handing(i, (0, 1, 2)):
            copy.wait_send()
        for j in range(half):
            for copy in reach(i, j):
                copy.wait_send()

    each(1, n, finish)
    for j in range(1, half):
        for copy in reach(0, j):
            copy.wait_send()
    for copy in heads + folds + wide + back + swaps:
        copy.wait_send()


def write_kernel(gradient, blocks, gradient_out, blocks_out, out_sem):
    def cut(ref, count):
        step = ref.shape[1] // count
        return [ref.at[:, pl.ds(c * step, step)] for c in range(count)]

    jobs = list(zip(cut(blocks, 2), cut(blocks_out, 2)))
    jobs += list(zip(cut(gradient, 4), cut(gradient_out, 4)))
    writes = [pltpu.make_async_copy(job[0], job[1], out_sem.at[j]) for j, job in enumerate(jobs)]
    for write in writes:
        write.start()
    for write in writes:
        write.wait()


def local(jacobians, residuals, camera_local, bucket_counts, camera_map):
    n, m = lax.axis_size("obs"), lax.axis_size("rep")
    slots = jacobians.shape[1]
    cap = slots // n
    cams = camera_map.shape[0]
    width = CAM_DEV // m
    highs = cams // LOW
    half = m // PAIR
    dma = pltpu.SemaphoreType.DMA
    early = n * LOW * CAM_DEV * 2 <= 8 * MIB
    kept = n if early else 1
    held = 16 * cams * 4 + 88 * CAM_DEV * 4
    limit = 60 * MIB - max(0, held - 2 * MIB)
    gradient, out = pl.pallas_call(
        functools.partial(main_kernel, n, m),
        out_shape=(VMEM((9, cams), F32), VMEM((81, CAM_DEV), F32)),
        in_specs=[pl.BlockSpec(memory_space=pltpu.SMEM)] + [pl.BlockSpec(memory_space=pltpu.HBM)] * 4,
        out_specs=(vspec(), vspec()),
        scratch_shapes=[
            VMEM((18, slots), F32),
            VMEM((2, slots), F32),
            VMEM((1, slots), jnp.int32),
            VMEM((1, cams), jnp.int32),
            dma((4,)),
            VMEM((4, slots), F32),
            VMEM((1, slots), F32),
            VMEM((n, 16, cap), F32),
            VMEM((n, 4, cap), F32),
            VMEM((n, 1, cap), F32),
            VMEM((kept, width, cap), BF16),
            VMEM((ROWS, cap), F32),
            VMEM((m, ROWS, width), F32),
            VMEM((half, KEPT, width), F32),
            VMEM((half, half, KEPT, width), F32),
            VMEM((half, KEPT, width), F32),
            VMEM((m, KEPT, width), F32),
            VMEM((m, 8, width), F32),
            VMEM((m, 1, width), F32),
            VMEM((m, 8, width), F32),
            VMEM((m, 1, width), F32),
            VMEM((8, width), F32),
            VMEM((1, width), F32),
            VMEM((half, n, 8, width), F32),
            VMEM((half, n, 1, width), F32),
            VMEM((kept, LOW, half * width), BF16),
            VMEM((highs * 18, LOW), F32),
            VMEM((8, cams), F32),
            VMEM((1, cams), F32),
            VMEM((8, cams), F32),
            VMEM((1, cams), F32),
            dma((3, n)),
            dma((3, n)),
            dma((2, m)),
            dma((2, m)),
            dma((2, n, half)),
            dma((2, n, half)),
            dma((2, CUTS)),
            dma((2, CUTS)),
            dma((half,)),
            dma((half,)),
            dma((half, half)),
            dma((half, half)),
            dma((half,)),
            dma((half,)),
        ],
        compiler_params=pltpu.CompilerParams(collective_id=0, has_side_effects=True, vmem_limit_bytes=limit),
    )(bucket_counts, jacobians, residuals, camera_local.reshape(1, slots), camera_map.reshape(1, cams))
    anywhere = pl.BlockSpec(memory_space=pl.ANY)
    shapes = (jax.ShapeDtypeStruct(gradient.shape, F32), jax.ShapeDtypeStruct(out.shape, F32))
    return pl.pallas_call(
        write_kernel,
        out_shape=shapes,
        in_specs=[vspec()] * 2,
        out_specs=(anywhere, anywhere),
        scratch_shapes=[dma((6,))],
        compiler_params=pltpu.CompilerParams(vmem_limit_bytes=2 * MIB),
    )(gradient, out)


def solution(mesh):
    in_specs = (
        P(None, ("obs", "rep")),
        P(None, ("obs", "rep")),
        P(("obs", "rep")),
        P(("obs", "rep"), None),
        P(),
    )
    out_specs = (P(), P(None, "obs"))
    return jax.shard_map(local, mesh=mesh, in_specs=in_specs, out_specs=out_specs, check_vma=False)
```

time: 33.9 us -> 30.1 us (0.89)
  Pallas kernels: 33.2 us -> 29.2 us
    pallas_call x1, Pallas kernels: 32.2 us -> 28.2 us  [local(): pl.pallas_call(functools.partial(main_kernel, n, m), out_shape=(VMEM((9,...]
where the time goes in v2:
time: 30.1 us; the launch traced here: 29.8 us
  Pallas kernels  29.2 us (97%)
  between operations  0.64 us (2%)
    pallas_call x1, Pallas kernels, local(): pl.pallas_call(functools.partial(main_kernel, n, m), out_shape=(VMEM((9,...  28.2 us
    pallas_call x1, Pallas kernels, local(): pl.pallas_call(write_kernel, out_shape=shapes, in_specs=[vspec()] * 2, ou...  0.96 us

profile of v2, /device:TPU:0, one launch (start us, length us, event | category | flops | bytes accessed | tf_op | source)
XLA Modules:
  0.0 29.8 jit_solution(1199742722990126168)
XLA Ops:
  0.6 28.2 %shard_map.68 = (f32[9,8192]{1,0:T(8,128)S(1)}, f32[81,1024]{1,0:T(8,128)S(1)}) custom-call(s32[1,8]{1,0:T(1,128)} %counts.1, f32[18,4096]{1,0:T(8,128)} %jac_in.1, f32[2,4096]{1,0:T(2,128)} %res_in.1, s32[1,4096]{1,0:T(1,128)} %bitcast.3, s32[1,8192]{1,0:T(1,128)} %bitcast.2), custom_call_target="tpu_custom_call" | custom-call | tf_op jit(solution)/shard_map/pallas_call | solution.py:409
  28.9 1.0 %shard_map.69 = (f32[9,8192]{1,0:T(8,128)}, f32[81,1024]{1,0:T(8,128)}) custom-call(f32[9,8192]{1,0:T(8,128)S(1)} %get-tuple-element.4.gradient, f32[81,1024]{1,0:T(8,128)S(1)} %get-tuple-element.5.blocks), custom_call_target="tpu_custom_call" | custom-call | tf_op jit(solution)/shard_map/pallas_call | solution.py:465

commit v3 on v2

--- a/solution.py
+++ b/solution.py
@@ -12,9 +12,10 @@
 F32 = jnp.float32
 BF16 = jnp.bfloat16
 VMEM = pltpu.VMEM
-ROWS = 56
 KEPT = 48
 CUTS = 4
+EARLY = 1
+INLINE = 1
 LOW = 256
 PAIR = 2
 MIB = 1024 * 1024
@@ -54,15 +55,18 @@
     return high, value - high
 
 
-def pack(counts, jac, res, ids, own4, own1):
+def pack(counts, jac, res, ids, tail, own4, own2, own8):
     buckets = counts.shape[1]
     cap = jac.shape[1] // buckets
+    tail[...] = jac[16:18, :]
     own4[0:2, :] = jac[16:18, :]
     own4[2:4, :] = res[...]
+    own8[...] = jac[0:8, :] * res[0:1, :] + jac[9:17, :] * res[1:2, :]
+    own2[1:2, :] = jac[8:9, :] * res[0:1, :] + jac[17:18, :] * res[1:2, :]
     place = lax.broadcasted_iota(jnp.int32, (1, cap), 1)
     for d in range(buckets):
         lanes = slice(d * cap, (d + 1) * cap)
-        own1[:, lanes] = jnp.where(place < counts[0, d], ids[:, lanes], -1).astype(F32)
+        own2[0:1, lanes] = jnp.where(place < counts[0, d], ids[:, lanes], -1).astype(F32)
 
 
 def one_hot_of(low, wide):
@@ -84,28 +88,37 @@
     return [jnp.where(up == jnp.asarray(h, BF16), value, zero) for h in range(pieces)]
 
 
-def add_block(most, four, ids, hot, terms, acc):
+def add_gradient(eight, pair, one_hot, acc, pieces):
+    up, _ = place_of(pair[0:1], acc.shape[1])
+    high, low = split(eight)
+    tiles = masked_tiles(jnp.concatenate([high, low], axis=0).astype(BF16), up, pieces)
+    high, low = split(pair[1:2])
+    mask = up == lax.broadcasted_iota(jnp.int32, (pieces, up.shape[1]), 0)
+    last = jnp.concatenate([jnp.where(mask, high, 0.0), jnp.where(mask, low, 0.0)], axis=0).astype(BF16)
+    lhs = jnp.concatenate(tiles + [last], axis=0)
+    acc[...] += lax.dot_general(lhs, one_hot, DIMS, preferred_element_type=F32)
+
+
+def add_block(most, two, ids, one_hot, terms, acc):
     pieces, _, width = acc.shape
-    lead, trail, res = most[0:9], jnp.concatenate([most[9:16], four[0:2]], axis=0), four[2:4]
-    at = 9
+    lead, trail = most[0:9], jnp.concatenate([most[9:16], two], axis=0)
+    at = 0
     for k in range(9):
         terms[at : at + 9 - k, :] = lead[k : k + 1] * lead[k:9] + trail[k : k + 1] * trail[k:9]
         at += 9 - k
-    terms[0:9, :] = lead * res[0:1] + trail * res[1:2]
     high, low = split(terms[...])
     both = jnp.concatenate([high, low], axis=0).astype(BF16)
-    up, down = place_of(ids, width)
-    one_hot = one_hot_of(down, width) if hot is None else hot[...]
+    up, _ = place_of(ids, width)
     lhs = jnp.concatenate(masked_tiles(both, up, pieces), axis=0)
     added = lax.dot_general(lhs, one_hot, DIMS, preferred_element_type=F32)
     for h in range(pieces):
-        at = h * 2 * ROWS
-        acc[h] += added[at : at + ROWS] + added[at + ROWS : at + 2 * ROWS]
+        at = h * 2 * KEPT
+        acc[h] += added[at : at + KEPT] + added[at + KEPT : at + 2 * KEPT]
 
 
 def expand(blocks, out):
     m, _, width = blocks.shape
-    at = 1
+    at = 0
     for k in range(9):
         for l in range(k, 9):
             for r in range(m):
@@ -170,13 +183,13 @@
 
 def main_kernel(
     n, m, counts, jac_in, res_in, ids_in, cmap_in, gradient, out, jac, res, ids, cmap, load_sem,
-    own4, own1, got16, got4, got1, hots, terms, part, fold, landed, total, blocks,
+    tail, own4, own2, own8, got16, got4, got2, got8, late16, late2, hots, terms, gsum, part, fold, landed, total, blocks,
     part8, part9, land8, land9, mine8, mine9, grads8, grads9, ready, spread, out8, out9, sib8, sib9,
     x_send, x_recv, a_send, a_recv, g_send, g_recv, c_send, c_recv, b_send, b_recv, w_send, w_recv, d_send, d_recv,
 ):
     me, rep = lax.axis_index("obs"), lax.axis_index("rep")
     width = total.shape[2]
-    cap = got16.shape[2]
+    cap, cut = got2.shape[2], got16.shape[2]
     half = m // PAIR
     sibling = rep + 1 - 2 * lax.rem(rep, PAIR)
     barrier = pltpu.get_barrier_semaphore()
@@ -195,20 +208,24 @@
         load.start()
     part[...] = jnp.zeros_like(part)
     terms[...] = jnp.zeros_like(terms)
+    gsum[...] = jnp.zeros_like(gsum)
     spread[...] = jnp.zeros_like(spread)
     for load in loads:
         load.wait()
-    pack(counts, jac, res, ids, own4, own1)
+    pack(counts, jac, res, ids, tail, own4, own2, own8)
     pl.semaphore_wait(barrier, n + m - 2)
 
-    def lanes_of(peer):
-        return pl.ds(pl.multiple_of(peer * cap, cap), cap)
+    def lanes_of(peer, first, count):
+        return pl.ds(pl.multiple_of(peer * cap + first, 128), count)
 
     def handing(i, kinds):
         peer = flip(i)
-        lanes = lanes_of(peer)
-        sent = (own1.at[:, lanes], jac.at[0:16, lanes], own4.at[:, lanes])
-        taken = (got1.at[i], got16.at[i], got4.at[i])
+        low, high = lanes_of(peer, 0, cut), lanes_of(peer, cut, cap - cut)
+        sent = (
+            own2.at[:, lanes_of(peer, 0, cap)], jac.at[0:16, low], own4.at[:, low], own8.at[:, high],
+            jac.at[0:16, high], tail.at[:, high],
+        )
+        taken = (got2.at[i], got16.at[i], got4.at[i], got8.at[i], late16.at[i], late2.at[i])
         return [
             pltpu.make_async_remote_copy(
                 src_ref=sent[k], dst_ref=taken[k], send_sem=x_send.at[k, i], recv_sem=x_recv.at[k, i],
@@ -225,40 +242,79 @@
         each(1, n, one)
 
     start((0,))
-    start((1, 2))
+    start((1, 2, 3))
     early = ready.shape[0] == n
+    side = lax.rem(rep, PAIR)
 
     def hot_at(i):
-        return hots.at[i] if early else None
-
-    side = lax.rem(rep, PAIR)
+        return hots.at[i if early else 0]
 
     def prepare(o, carry):
         ready[o] = one_hot_of(lax.rem(side_ids(o, side, half, cmap, width), LOW), LOW)
         return carry
+
+    def see(i):
+        hot_at(i)[...] = one_hot_of(place_of(got2[i, 0:1], width)[1], width)
 
     def foresee(i, carry):
         for copy in handing(i, (0,)):
             copy.wait_recv()
         if early:
-            hots[i] = one_hot_of(place_of(got1[i], width)[1], width)
-        return carry
+            see(i)
+        return carry
+
+    def gradient_of(i):
+        most, four = got16[i], got4[i]
+        trail = jnp.concatenate([most[9:16], four[0:2]], axis=0)
+        near = most[0:9] * four[2:3] + trail * four[3:4]
+        eight = jnp.concatenate([near[0:8], got8[i]], axis=1)
+        ninth = jnp.concatenate([near[8:9], got2[i, 1:2, cut:]], axis=1)
+        add_gradient(eight, jnp.concatenate([got2[i, 0:1], ninth], axis=0), hot_at(i)[...], gsum, m)
+
+    def low_block(i):
+        if not early:
+            see(i)
+        add_block(got16[i], got4[i, 0:2], got2[i, 0:1, 0:cut], hot_at(i)[:, 0:cut], terms.at[:, 0:cut], part)
 
     def take(i, carry):
-        for copy in handing(i, (1, 2)):
+        for copy in handing(i, (1, 2, 3)):
             copy.wait_recv()
-        add_block(got16[i], got4[i], got1[i], hot_at(i), terms, part)
-        return carry
-
-    mylanes = lanes_of(me)
-    add_block(jac[0:16, mylanes], own4[:, mylanes], own1[:, mylanes], None, terms, part)
+        if not early:
+            see(i)
+        gradient_of(i)
+        return carry
+
+    def take_both(i, carry):
+        take(i, carry)
+        low_block(i)
+        return carry
+
+    def take_low(i, carry):
+        low_block(i)
+        return carry
+
+    def take_late(i, carry):
+        for copy in handing(i, (4, 5)):
+            copy.wait_recv()
+        if not early:
+            see(i)
+        add_block(late16[i], late2[i], got2[i, 0:1, cut:], hot_at(i)[:, cut:], terms.at[:, 0 : cap - cut], part)
+        return carry
+
+    mylanes = lanes_of(me, 0, cap)
+    hot_at(0)[...] = one_hot_of(place_of(own2[0:1, mylanes], width)[1], width)
+    add_gradient(own8[:, mylanes], own2[:, mylanes], hot_at(0)[...], gsum, m)
+    add_block(jac[0:16, mylanes], tail[:, mylanes], own2[0:1, mylanes], hot_at(0)[...], terms, part)
     lax.fori_loop(1, n, foresee, 0)
     if early:
         lax.fori_loop(0, n, prepare, 0)
-    lax.fori_loop(1, n, take, 0)
+    inline = min(INLINE, n)
+    lax.fori_loop(1, inline, take_both, 0)
+    lax.fori_loop(inline, n, take, 0)
     for h in range(m):
-        part8[h] = part[h, 0:8]
-        part9[h] = part[h, 8:9]
+        part8[h] = gsum[h * 16 : h * 16 + 8, :] + gsum[h * 16 + 8 : h * 16 + 16, :]
+        ninth = m * 16 + h
+        part9[h] = gsum[ninth : ninth + 1, :] + gsum[ninth + m : ninth + m + 1, :]
 
     def to_rep(src, dst, s, r, peer):
         return pltpu.make_async_remote_copy(
@@ -272,16 +328,9 @@
         heads.append(to_rep(part9.at[peer], land9.at[i], a_send.at[1, i], a_recv.at[1, i], peer))
     for copy in heads:
         copy.start()
-    mine_at, other_at = side * half, (1 - side) * half
-    folds, wide, back = [], [], []
-    for h in range(half):
-        folds.append(to_rep(part.at[other_at + h, pl.ds(ROWS - KEPT, KEPT)], fold.at[h], b_send.at[h], b_recv.at[h], sibling))
-        for j in range(1, half):
-            peer = lax.rem(rep + PAIR * j, m)
-            wide.append(to_rep(total.at[h], landed.at[j, h], w_send.at[j, h], w_recv.at[j, h], peer))
-        back.append(to_rep(blocks.at[mine_at + h], blocks.at[mine_at + h], d_send.at[h], d_recv.at[h], sibling))
-    for copy in folds:
-        copy.start()
+    start((4, 5))
+    lax.fori_loop(inline, n, take_low, 0)
+    lax.fori_loop(1, min(EARLY, n), take_late, 0)
     for copy in heads:
         copy.wait_recv()
     eight, ninth = part8[rep], part9[rep]
@@ -330,9 +379,20 @@
         place(i, 0)
         return carry
 
+    lax.fori_loop(min(EARLY, n), n, take_late, 0)
+    mine_at, other_at = side * half, (1 - side) * half
+    folds, wide, back = [], [], []
+    for h in range(half):
+        folds.append(to_rep(part.at[other_at + h], fold.at[h], b_send.at[h], b_recv.at[h], sibling))
+        for j in range(1, half):
+            peer = lax.rem(rep + PAIR * j, m)
+            wide.append(to_rep(total.at[h], landed.at[j, h], w_send.at[j, h], w_recv.at[j, h], peer))
+        back.append(to_rep(blocks.at[mine_at + h], blocks.at[mine_at + h], d_send.at[h], d_recv.at[h], sibling))
+    for copy in folds:
+        copy.start()
     for h in range(half):
         folds[h].wait_recv()
-        total[h] = part[mine_at + h, ROWS - KEPT :] + fold[h]
+        total[h] = part[mine_at + h] + fold[h]
         for copy in wide[h * (half - 1) : (h + 1) * (half - 1)]:
             copy.start()
     place(0, 1)
@@ -365,7 +425,7 @@
     expand(blocks, out)
 
     def finish(i):
-        for copy in handing(i, (0, 1, 2)):
+        for copy in handing(i, (0, 1, 2, 3, 4, 5)):
             copy.wait_send()
         for j in range(half):
             for copy in reach(i, j):
@@ -397,6 +457,7 @@
     n, m = lax.axis_size("obs"), lax.axis_size("rep")
     slots = jacobians.shape[1]
     cap = slots // n
+    cut = cap // 2
     cams = camera_map.shape[0]
     width = CAM_DEV // m
     highs = cams // LOW
@@ -417,14 +478,20 @@
             VMEM((1, slots), jnp.int32),
             VMEM((1, cams), jnp.int32),
             dma((4,)),
+            VMEM((2, slots), F32),
             VMEM((4, slots), F32),
-            VMEM((1, slots), F32),
-            VMEM((n, 16, cap), F32),
-            VMEM((n, 4, cap), F32),
-            VMEM((n, 1, cap), F32),
+            VMEM((2, slots), F32),
+            VMEM((8, slots), F32),
+            VMEM((n, 16, cut), F32),
+            VMEM((n, 4, cut), F32),
+            VMEM((n, 2, cap), F32),
+            VMEM((n, 8, cap - cut), F32),
+            VMEM((n, 16, cap - cut), F32),
+            VMEM((n, 2, cap - cut), F32),
             VMEM((kept, width, cap), BF16),
-            VMEM((ROWS, cap), F32),
-            VMEM((m, ROWS, width), F32),
+            VMEM((KEPT, cap), F32),
+            VMEM((m * 18, width), F32),
+            VMEM((m, KEPT, width), F32),
             VMEM((half, KEPT, width), F32),
             VMEM((half, half, KEPT, width), F32),
             VMEM((half, KEPT, width), F32),
@@ -443,8 +510,8 @@
             VMEM((1, cams), F32),
             VMEM((8, cams), F32),
             VMEM((1, cams), F32),
-            dma((3, n)),
-            dma((3, n)),
+            dma((6, n)),
+            dma((6, n)),
             dma((2, m)),
             dma((2, m)),
             dma((2, n, half)),

time: 30.1 us -> 29.2 us (0.970)
  Pallas kernels: 29.2 us -> 28.3 us
    pallas_call x1, Pallas kernels: 28.2 us -> 27.3 us  [local(): pl.pallas_call(functools.partial(main_kernel, n, m), out_shape=(VMEM((9,...]
where the time goes in v3:
time: 29.2 us; the launch traced here: 28.9 us
  Pallas kernels  28.3 us (97%)
  between operations  0.64 us (2%)
    pallas_call x1, Pallas kernels, local(): pl.pallas_call(functools.partial(main_kernel, n, m), out_shape=(VMEM((9,...  27.3 us
    pallas_call x1, Pallas kernels, local(): pl.pallas_call(write_kernel, out_shape=shapes, in_specs=[vspec()] * 2, ou...  0.96 us

profile of v3, /device:TPU:0, one launch (start us, length us, event | category | flops | bytes accessed | tf_op | source)
XLA Modules:
  0.0 28.9 jit_solution(17880128434542557014)
XLA Ops:
  0.6 27.3 %shard_map.68 = (f32[9,8192]{1,0:T(8,128)S(1)}, f32[81,1024]{1,0:T(8,128)S(1)}) custom-call(s32[1,8]{1,0:T(1,128)} %counts.1, f32[18,4096]{1,0:T(8,128)} %jac_in.1, f32[2,4096]{1,0:T(2,128)} %res_in.1, s32[1,4096]{1,0:T(1,128)} %bitcast.3, s32[1,8192]{1,0:T(1,128)} %bitcast.2), custom_call_target="tpu_custom_call" | custom-call | tf_op jit(solution)/shard_map/pallas_call | solution.py:470
  27.9 1.0 %shard_map.69 = (f32[9,8192]{1,0:T(8,128)}, f32[81,1024]{1,0:T(8,128)}) custom-call(f32[9,8192]{1,0:T(8,128)S(1)} %get-tuple-element.4.gradient, f32[81,1024]{1,0:T(8,128)S(1)} %get-tuple-element.5.blocks), custom_call_target="tpu_custom_call" | custom-call | tf_op jit(solution)/shard_map/pallas_call | solution.py:532

commit v4 on v3

--- a/solution.py
+++ b/solution.py
@@ -13,7 +13,7 @@
 BF16 = jnp.bfloat16
 VMEM = pltpu.VMEM
 KEPT = 48
-CUTS = 4
+CUTS = 2
 EARLY = 1
 INLINE = 1
 LOW = 256
@@ -184,7 +184,7 @@
 def main_kernel(
     n, m, counts, jac_in, res_in, ids_in, cmap_in, gradient, out, jac, res, ids, cmap, load_sem,
     tail, own4, own2, own8, got16, got4, got2, got8, late16, late2, hots, terms, gsum, part, fold, landed, total, blocks,
-    part8, part9, land8, land9, mine8, mine9, grads8, grads9, ready, spread, out8, out9, sib8, sib9,
+    part8, part9, land8, land9, mine, grads, ready, spread, out8, out9, sib8, sib9,
     x_send, x_recv, a_send, a_recv, g_send, g_recv, c_send, c_recv, b_send, b_recv, w_send, w_recv, d_send, d_recv,
 ):
     me, rep = lax.axis_index("obs"), lax.axis_index("rep")
@@ -199,7 +199,7 @@
     def greet(i):
         pl.semaphore_signal(barrier, inc=1, device_id={"obs": flip(i)}, device_id_type=MESH)
 
-    each(1, n, greet)
+    each(1, n, lambda i: greet(n - i))
     for i in range(1, m):
         pl.semaphore_signal(barrier, inc=1, device_id={"rep": lax.rem(rep + i, m)}, device_id_type=MESH)
     pairs = ((jac_in, jac), (res_in, res), (ids_in, ids), (cmap_in, cmap))
@@ -234,15 +234,16 @@
             for k in kinds
         ]
 
-    def start(kinds):
+    def start(kinds, first, last):
         def one(i):
-            for copy in handing(n - i, kinds):
+            for copy in handing(first + last - 1 - i, kinds):
                 copy.start()
 
-        each(1, n, one)
-
-    start((0,))
-    start((1, 2, 3))
+        each(first, last, one)
+
+    start((0,), 1, n)
+    start((1, 2, 3), 2, n)
+    start((1, 2, 3, 4, 5), 1, 2)
     early = ready.shape[0] == n
     side = lax.rem(rep, PAIR)
 
@@ -328,7 +329,7 @@
         heads.append(to_rep(part9.at[peer], land9.at[i], a_send.at[1, i], a_recv.at[1, i], peer))
     for copy in heads:
         copy.start()
-    start((4, 5))
+    start((4, 5), 2, n)
     lax.fori_loop(inline, n, take_low, 0)
     lax.fori_loop(1, min(EARLY, n), take_late, 0)
     for copy in heads:
@@ -337,22 +338,18 @@
     for i in range(1, m):
         eight = eight + land8[i]
         ninth = ninth + land9[i]
-    mine8[...] = eight
-    mine9[...] = ninth
-    grads8[lax.div(rep, PAIR), me] = eight
-    grads9[lax.div(rep, PAIR), me] = ninth
-
-    def at_origin(origin, source):
-        return grads8.at[origin, source], grads9.at[origin, source]
+    for k in range(9):
+        row = eight[k : k + 1] if k < 8 else ninth
+        mine[k] = row
+        grads[lax.div(rep, PAIR), me, k] = row
 
     def reach(i, j):
         where = {"obs": flip(i), "rep": lax.rem(rep + PAIR * j, m)}
         return [
             pltpu.make_async_remote_copy(
-                src_ref=src, dst_ref=dst, send_sem=g_send.at[k, i, j], recv_sem=g_recv.at[k, i, j],
-                device_id=where, device_id_type=MESH,
+                src_ref=mine, dst_ref=grads.at[lax.div(rep, PAIR), me], send_sem=g_send.at[i, j],
+                recv_sem=g_recv.at[i, j], device_id=where, device_id_type=MESH,
             )
-            for k, (src, dst) in enumerate(zip((mine8, mine9), at_origin(lax.div(rep, PAIR), me)))
         ]
 
     def spread_out(i):
@@ -370,8 +367,8 @@
         for j in range(first, half):
             for copy in reach(i, j):
                 copy.wait_recv()
-        eight = jnp.concatenate([grads8[j, source] for j in range(half)], axis=1)
-        ninth = jnp.concatenate([grads9[j, source] for j in range(half)], axis=1)
+        rows = [jnp.concatenate([grads[j, source, k] for j in range(half)], axis=1) for k in range(9)]
+        eight, ninth = jnp.concatenate(rows[0:8], axis=0), rows[8]
         here = side_ids(source, side, half, cmap, width)
         place_chunk(eight, ninth, here, ready[source] if early else None, spread)
 
@@ -395,6 +392,18 @@
         total[h] = part[mine_at + h] + fold[h]
         for copy in wide[h * (half - 1) : (h + 1) * (half - 1)]:
             copy.start()
+    def drain(i):
+        for copy in handing(i, (0, 1, 2, 3, 4, 5)):
+            copy.wait_send()
+
+    def drain_reach(i):
+        for j in range(half):
+            for copy in reach(i, j):
+                copy.wait_send()
+
+    each(1, n, drain)
+    for copy in heads + folds:
+        copy.wait_send()
     place(0, 1)
     lax.fori_loop(1, n, settle, 0)
     swaps = []
@@ -406,6 +415,10 @@
         swaps.append(to_rep(out9.at[:, lanes], sib9.at[:, lanes], c_send.at[1, c], c_recv.at[1, c], sibling))
         for copy in swaps[-2:]:
             copy.start()
+    each(1, n, drain_reach)
+    for j in range(1, half):
+        for copy in reach(0, j):
+            copy.wait_send()
     for h in range(half):
         for copy in wide[h * (half - 1) : (h + 1) * (half - 1)]:
             copy.wait_recv()
@@ -414,6 +427,8 @@
             full = full + landed[j, h]
         blocks[mine_at + h] = full
         back[h].start()
+    for copy in wide:
+        copy.wait_send()
     for c in range(CUTS):
         lanes = slice(c * step, (c + 1) * step)
         for copy in swaps[2 * c : 2 * c + 2]:
@@ -424,18 +439,7 @@
         copy.wait_recv()
     expand(blocks, out)
 
-    def finish(i):
-        for copy in handing(i, (0, 1, 2, 3, 4, 5)):
-            copy.wait_send()
-        for j in range(half):
-            for copy in reach(i, j):
-                copy.wait_send()
-
-    each(1, n, finish)
-    for j in range(1, half):
-        for copy in reach(0, j):
-            copy.wait_send()
-    for copy in heads + folds + wide + back + swaps:
+    for copy in back + swaps:
         copy.wait_send()
 
 
@@ -500,10 +504,8 @@
             VMEM((m, 1, width), F32),
             VMEM((m, 8, width), F32),
             VMEM((m, 1, width), F32),
-            VMEM((8, width), F32),
-            VMEM((1, width), F32),
-            VMEM((half, n, 8, width), F32),
-            VMEM((half, n, 1, width), F32),
+            VMEM((9, 1, width), F32),
+            VMEM((half, n, 9, 1, width), F32),
             VMEM((kept, LOW, half * width), BF16),
             VMEM((highs * 18, LOW), F32),
             VMEM((8, cams), F32),
@@ -514,8 +516,8 @@
             dma((6, n)),
             dma((2, m)),
             dma((2, m)),
-            dma((2, n, half)),
-            dma((2, n, half)),
+            dma((n, half)),
+            dma((n, half)),
             dma((2, CUTS)),
             dma((2, CUTS)),
             dma((half,)),

time: 29.2 us -> 28.7 us (0.983)
  Pallas kernels: 28.3 us -> 27.9 us
    pallas_call x1, Pallas kernels: 27.3 us -> 26.9 us  [local(): pl.pallas_call(functools.partial(main_kernel, n, m), out_shape=(VMEM((9,...]
where the time goes in v4:
time: 28.7 us; the launch traced here: 28.5 us
  Pallas kernels  27.9 us (97%)
  between operations  0.64 us (2%)
    pallas_call x1, Pallas kernels, local(): pl.pallas_call(functools.partial(main_kernel, n, m), out_shape=(VMEM((9,...  26.9 us
    pallas_call x1, Pallas kernels, local(): pl.pallas_call(write_kernel, out_shape=shapes, in_specs=[vspec()] * 2, ou...  0.96 us

profile of v4, /device:TPU:0, one launch (start us, length us, event | category | flops | bytes accessed | tf_op | source)
XLA Modules:
  0.0 28.5 jit_solution(17984559138039294822)
XLA Ops:
  0.6 26.9 %shard_map.68 = (f32[9,8192]{1,0:T(8,128)S(1)}, f32[81,1024]{1,0:T(8,128)S(1)}) custom-call(s32[1,8]{1,0:T(1,128)} %counts.1, f32[18,4096]{1,0:T(8,128)} %jac_in.1, f32[2,4096]{1,0:T(2,128)} %res_in.1, s32[1,4096]{1,0:T(1,128)} %bitcast.3, s32[1,8192]{1,0:T(1,128)} %bitcast.2), custom_call_target="tpu_custom_call" | custom-call | tf_op jit(solution)/shard_map/pallas_call | solution.py:474
  27.6 1.0 %shard_map.69 = (f32[9,8192]{1,0:T(8,128)}, f32[81,1024]{1,0:T(8,128)}) custom-call(f32[9,8192]{1,0:T(8,128)S(1)} %get-tuple-element.4.gradient, f32[81,1024]{1,0:T(8,128)S(1)} %get-tuple-element.5.blocks), custom_call_target="tpu_custom_call" | custom-call | tf_op jit(solution)/shard_map/pallas_call | solution.py:534

commit v5 on v4

--- a/solution.py
+++ b/solution.py
@@ -13,7 +13,7 @@
 BF16 = jnp.bfloat16
 VMEM = pltpu.VMEM
 KEPT = 48
-CUTS = 2
+CUTS = 1
 EARLY = 1
 INLINE = 1
 LOW = 256
@@ -184,7 +184,7 @@
 def main_kernel(
     n, m, counts, jac_in, res_in, ids_in, cmap_in, gradient, out, jac, res, ids, cmap, load_sem,
     tail, own4, own2, own8, got16, got4, got2, got8, late16, late2, hots, terms, gsum, part, fold, landed, total, blocks,
-    part8, part9, land8, land9, mine, grads, ready, spread, out8, out9, sib8, sib9,
+    piece, land, mine, grads, ready, spread, out8, out9, sib8, sib9,
     x_send, x_recv, a_send, a_recv, g_send, g_recv, c_send, c_recv, b_send, b_recv, w_send, w_recv, d_send, d_recv,
 ):
     me, rep = lax.axis_index("obs"), lax.axis_index("rep")
@@ -313,9 +313,11 @@
     lax.fori_loop(1, inline, take_both, 0)
     lax.fori_loop(inline, n, take, 0)
     for h in range(m):
-        part8[h] = gsum[h * 16 : h * 16 + 8, :] + gsum[h * 16 + 8 : h * 16 + 16, :]
+        eight = gsum[h * 16 : h * 16 + 8, :] + gsum[h * 16 + 8 : h * 16 + 16, :]
         ninth = m * 16 + h
-        part9[h] = gsum[ninth : ninth + 1, :] + gsum[ninth + m : ninth + m + 1, :]
+        for k in range(8):
+            piece[h, k] = eight[k : k + 1]
+        piece[h, 8] = gsum[ninth : ninth + 1, :] + gsum[ninth + m : ninth + m + 1, :]
 
     def to_rep(src, dst, s, r, peer):
         return pltpu.make_async_remote_copy(
@@ -325,8 +327,7 @@
     heads = []
     for i in range(1, m):
         peer = lax.rem(rep + i, m)
-        heads.append(to_rep(part8.at[peer], land8.at[i], a_send.at[0, i], a_recv.at[0, i], peer))
-        heads.append(to_rep(part9.at[peer], land9.at[i], a_send.at[1, i], a_recv.at[1, i], peer))
+        heads.append(to_rep(piece.at[peer], land.at[i], a_send.at[i], a_recv.at[i], peer))
     for copy in heads:
         copy.start()
     start((4, 5), 2, n)
@@ -334,14 +335,11 @@
     lax.fori_loop(1, min(EARLY, n), take_late, 0)
     for copy in heads:
         copy.wait_recv()
-    eight, ninth = part8[rep], part9[rep]
+    summed = piece[rep]
     for i in range(1, m):
-        eight = eight + land8[i]
-        ninth = ninth + land9[i]
-    for k in range(9):
-        row = eight[k : k + 1] if k < 8 else ninth
-        mine[k] = row
-        grads[lax.div(rep, PAIR), me, k] = row
+        summed = summed + land[i]
+    mine[...] = summed
+    grads[lax.div(rep, PAIR), me] = summed
 
     def reach(i, j):
         where = {"obs": flip(i), "rep": lax.rem(rep + PAIR * j, m)}
@@ -354,7 +352,7 @@
 
     def spread_out(i):
         for j in reversed(range(half)):
-            for copy in reach(n - i, j):
+            for copy in reach(i, j):
                 copy.start()
 
     each(1, n, spread_out)
@@ -500,10 +498,8 @@
             VMEM((half, half, KEPT, width), F32),
             VMEM((half, KEPT, width), F32),
             VMEM((m, KEPT, width), F32),
-            VMEM((m, 8, width), F32),
-            VMEM((m, 1, width), F32),
-            VMEM((m, 8, width), F32),
-            VMEM((m, 1, width), F32),
+            VMEM((m, 9, 1, width), F32),
+            VMEM((m, 9, 1, width), F32),
             VMEM((9, 1, width), F32),
             VMEM((half, n, 9, 1, width), F32),
             VMEM((kept, LOW, half * width), BF16),
@@ -514,8 +510,8 @@
             VMEM((1, cams), F32),
             dma((6, n)),
             dma((6, n)),
-            dma((2, m)),
-            dma((2, m)),
+            dma((m,)),
+            dma((m,)),
             dma((n, half)),
             dma((n, half)),
             dma((2, CUTS)),

time: 28.7 us -> 28.5 us (level)
  no operation moved by 1% of the time
where the time goes in v5:
time: 28.5 us; the launch traced here: 28.4 us
  Pallas kernels  27.7 us (97%)
  between operations  0.64 us (2%)
    pallas_call x1, Pallas kernels, local(): pl.pallas_call(functools.partial(main_kernel, n, m), out_shape=(VMEM((9,...  26.8 us
    pallas_call x1, Pallas kernels, local(): pl.pallas_call(write_kernel, out_shape=shapes, in_specs=[vspec()] * 2, ou...  0.96 us

profile of v5, /device:TPU:0, one launch (start us, length us, event | category | flops | bytes accessed | tf_op | source)
XLA Modules:
  0.0 28.4 jit_solution(2424876357988201352)
XLA Ops:
  0.6 26.8 %shard_map.68 = (f32[9,8192]{1,0:T(8,128)S(1)}, f32[81,1024]{1,0:T(8,128)S(1)}) custom-call(s32[1,8]{1,0:T(1,128)} %counts.1, f32[18,4096]{1,0:T(8,128)} %jac_in.1, f32[2,4096]{1,0:T(2,128)} %res_in.1, s32[1,4096]{1,0:T(1,128)} %bitcast.3, s32[1,8192]{1,0:T(1,128)} %bitcast.2), custom_call_target="tpu_custom_call" | custom-call | tf_op jit(solution)/shard_map/pallas_call | solution.py:472
  27.4 1.0 %shard_map.69 = (f32[9,8192]{1,0:T(8,128)}, f32[81,1024]{1,0:T(8,128)}) custom-call(f32[9,8192]{1,0:T(8,128)S(1)} %get-tuple-element.4.gradient, f32[81,1024]{1,0:T(8,128)S(1)} %get-tuple-element.5.blocks), custom_call_target="tpu_custom_call" | custom-call | tf_op jit(solution)/shard_map/pallas_call | solution.py:530
